TPU v7x, 32 devices: a whole 2x2x4 slice. The times are simulated.
32 devices in a mesh: row: 8 (over z, y), col: 4 (over x, core).
Axes of the slice: x: 2, y: 2, z: 4, core: 2. Of those that a mesh axis runs over, the one named last changes fastest.
Arguments:
- features: float32 [32, 3072], P(None, ('row', 'col')), may hold values from -6 to 6
- block: float32 [16, 3072], P(None, ('row', 'col')), may hold values from -6 to 6
Outputs:
- applied: float32 [16, 3072], P(None, ('row', 'col'))
All inputs are finite; a program needn't handle non-finite values.
Results may differ from a plain program's by a relative error of at most 0.006.
Values may be sent and summed in bfloat16 or wider, within the bound.
A program may use at most 64 MiB of HBM per device.

v0:
```python
import math
import jax
import jax.numpy as jnp
from jax import lax
from jax.sharding import PartitionSpec as P


def kernel_rows(row_feat, row_sq, col_feat, col_sq, scale, start, count):
    part = lax.dynamic_slice_in_dim(row_feat, start, count, 1)
    sq_part = lax.dynamic_slice_in_dim(row_sq, start, count, 0)
    inner = jnp.einsum("fi,fj->ij", part, col_feat, precision=lax.Precision.HIGHEST)
    dist = sq_part[:, None] + col_sq[None, :] - 2.0 * inner
    return jnp.exp(-dist / scale).astype(jnp.bfloat16)


def combine(partial_value, owned):
    whole = lax.psum(partial_value, "col")
    return lax.dynamic_slice_in_dim(whole, lax.axis_index("col") * owned, owned, 1)


def full_plan(features, block, row_feat, scale):
    owned = features.shape[1]
    col_feat = lax.all_gather(features, "row", axis=1, tiled=True)
    row_sq = jnp.sum(row_feat * row_feat, axis=0)
    col_sq = jnp.sum(col_feat * col_feat, axis=0)
    rows = row_feat.shape[1]
    step = math.gcd(512, rows)
    count_blocks = rows // step
    starts = jnp.arange(count_blocks, dtype=jnp.int32) * step
    indexes = jnp.arange(count_blocks, dtype=jnp.int32)

    def fetch(index):
        return kernel_rows(row_feat, row_sq, col_feat, col_sq, scale, starts[index], step)

    def first_pass(index):
        tile = fetch(index)
        return (jnp.sum(tile, axis=1, dtype=jnp.float32), jnp.sum(tile, axis=0, dtype=jnp.float32))

    row_parts, col_parts = lax.map(first_pass, indexes)
    q_own = combine(row_parts.reshape(1, rows), owned)
    inv_own = 1.0 / q_own
    col_total = lax.psum(jnp.sum(col_parts, axis=0)[None, :], "row")
    inv_col = 1.0 / col_total

    def second_pass(index):
        return jnp.sum(fetch(index).astype(jnp.float32) * inv_col, axis=1)

    second = combine(lax.map(second_pass, indexes).reshape(1, rows), owned)
    dens = second * inv_own
    factor = inv_own * lax.rsqrt(dens)
    weighted = (block * factor).astype(jnp.bfloat16)
    weighted_col = lax.all_gather(weighted, "row", axis=1, tiled=True)

    def third_pass(index):
        return jnp.einsum(
            "kj,ij->ki", weighted_col, fetch(index), preferred_element_type=jnp.float32
        )

    products = lax.map(third_pass, indexes)
    partial_value = jnp.moveaxis(products, 0, 1).reshape(block.shape[0], rows)
    return combine(partial_value, owned) * factor


def per_device(features, block):
    n_row = lax.axis_size("row")
    n_col = lax.axis_size("col")
    width, owned = features.shape
    frames = owned * n_row * n_col
    scale = 4.0 / (float(frames) ** (2.0 / width) - 1.0)
    row_feat = lax.all_gather(features, "col", axis=1, tiled=True)
    return full_plan(features, block, row_feat, scale)


def solution(mesh):
    placed = (P(None, ("row", "col")), P(None, ("row", "col")))
    return jax.shard_map(
        per_device, mesh=mesh, in_specs=placed, out_specs=P(None, ("row", "col")), check_vma=False
    )
```

profile of v0, /device:TPU:0, one launch (start us, length us, event | category | flops | bytes accessed | tf_op | source)
XLA Modules:
  0.0 166.0 jit_solution(17195008290931523014)
XLA Ops:
  0.0 32.5 %all-gather.1 = f32[8,96,32]{1,2,0:T(8,128)S(1)} all-gather(f32[1,96,32]{1,2,0:T(8,128)} %bitcast.84), channel_id=1, replica_groups=mesh['row'=8,'col'=4] {'row'}, dimensions={0}, use_global_device_ids=true | all-gather | bytes 110592 | tf_op jit(solution)/shard_map/all_gather | solution.py:23
  32.8 0.7 copy-done
  33.4 5.2 %all-gather = f32[4,96,32]{1,2,0:T(8,128)S(1)} all-gather(f32[1,96,32]{1,2,0:T(8,128)S(1)} %bitcast.85), channel_id=1, replica_groups=mesh['row'=8,'col'=4] {'col'}, dimensions={0}, use_global_device_ids=true | all-gather | bytes 61440 | tf_op jit(solution)/shard_map/all_gather | solution.py:70
  38.9 19.3 %while.32 = (s32[]{:T(128)}, f32[3,128]{1,0:T(4,128)S(1)}, f32[3,768]{1,0:T(4,128)S(1)}, s32[3]{0:T(128)S(1)}, s32[3]{0:T(128)S(1)}, /*index=5*/f32[384]{0:T(512...) while((s32[]{:T(128)}, f32[3,128]{1,0:T(4,128)S(1)}, ...), condition=%wide.region_5.6_spmd, body=%wide.region_2.5_spmd.sunk | while | flops 38632584 | bytes 137449 | solution.py:39
  41.6 0.7 dynamic_slice.88
  44.5 0.7 fusion.51
  45.3 0.7 dynamic_slice.87
  48.1 0.7 dynamic_slice.88
  50.9 0.7 fusion.51
  51.8 0.7 dynamic_slice.87
  54.5 0.7 dynamic_slice.88
  57.3 0.7 fusion.51
  58.2 21.4 %psum.29 = f32[1,768]{1,0:T(1,128)S(1)} all-reduce(f32[1,768]{1,0:T(1,128)S(1)} %broadcast_in_dim.32), channel_id=1, replica_groups=mesh['row'=8,'col'=4] {'row'}, use_global_device_ids=true, to_apply=%region_8.9 | all-reduce | flops 768 | bytes 6144 | tf_op jit(solution)/shard_map/psum | solution.py:42
  79.6 19.1 %while.33 = (s32[]{:T(128)}, f32[3,128]{1,0:T(4,128)S(1)}, s32[3]{0:T(128)S(1)}, s32[3]{0:T(128)S(1)}, f32[384]{0:T(512)S(1)}, /*index=5*/f32[768]{0:T(1024)S(1)...) while((s32[]{:T(128)}, f32[3,128]{1,0:T(4,128)S(1)}, ...), condition=%wide.region_11.12_spmd, body=%wide.region_9.11_spmd.sunk | while | flops 38633352 | bytes 132337 | solution.py:48
  79.6 0.7 dynamic_slice.91
  82.4 0.7 dynamic_slice.92
  85.2 0.7 fusion.54
  88.7 0.7 dynamic_slice.92
  91.6 0.7 fusion.54
  92.3 0.7 dynamic_slice.91
  95.1 0.7 dynamic_slice.92
  97.9 0.7 fusion.54
  98.7 5.7 %all-reduce = (f32[1,384]{1,0:T(1,128)S(1)}, f32[1,384]{1,0:T(1,128)S(1)}) all-reduce(f32[1,384]{1,0:T(1,128)S(1)} %get-tuple-element.209, f32[1,384]{1,0:T(1,128)S(1)} %get-tuple-element.210), channel_id=1, replica_groups=mesh['row'=8,'col'=4] {'col'}, use_global_device_ids=true, to_apply=%region_12.13 | all-reduce | flops 768 | bytes 6144 | tf_op jit(solution)/shard_map/psum | solution.py:17
  105.1 30.6 %all-gather.2 = bf16[8,96,16]{1,2,0:T(8,128)(2,1)S(1)} all-gather(bf16[1,96,16]{1,2,0:T(8,128)(2,1)S(1)} %fusion.26), channel_id=1, replica_groups=mesh['row'=8,'col'=4] {'row'}, dimensions={0}, use_global_device_ids=true | all-gather | bytes 27648 | tf_op jit(solution)/shard_map/all_gather | solution.py:52
  135.8 19.2 %while.34 = (s32[]{:T(128)}, f32[3,16,128]{2,1,0:T(8,128)S(1)}, s32[3]{0:T(128)S(1)}, s32[3]{0:T(128)S(1)}, f32[384]{0:T(512)S(1)}, /*index=5*/f32[768]{0:T(1024...) while((s32[]{:T(128)}, f32[3,16,128]{2,1,0:T(8,128)S(1)}, ...), condition=%wide.region_14.15_spmd, body=%wide.region_13.14_spmd.sunk | while | flops 41484296 | bytes 546533 | solution.py:59
  138.6 0.7 dynamic_slice.96
  142.2 0.7 dynamic_slice.95
  145.0 0.7 dynamic_slice.96
  148.6 0.7 dynamic_slice.95
  151.4 0.7 dynamic_slice.96
  155.0 10.3 %psum.31 = f32[16,384]{1,0:T(8,128)S(1)} all-reduce(f32[16,384]{1,0:T(8,128)S(1)} %copy_bitcast_fusion), channel_id=1, replica_groups=mesh['row'=8,'col'=4] {'col'}, use_global_device_ids=true, to_apply=%region_15.16 | all-reduce | flops 6144 | bytes 49152 | tf_op jit(solution)/shard_map/psum | solution.py:17
  165.3 0.7 dynamic-slice_multiply_fusion
  (59 shorter events, 6.7 us)
Async XLA Ops:
  32.7 0.7 copy-start
  104.4 0.7 copy-start.1
where the time goes:
time: 167 us; the launch traced here: 166 us
  blocking collectives  106 us (63%)
  loops' own time  37.5 us (22%)
  local copies, waits for them, and re-layouts  15 us (9%)
  matrix products  6.79 us (4%)
    all_gather x1, blocking collectives, full_plan(): col_feat = lax.all_gather(features, 'row', axis=1, tiled=True)  32.5 us
    all_gather x1, blocking collectives, full_plan(): weighted_col = lax.all_gather(weighted, 'row', axis=1, tiled=True)  30.6 us
    psum x1, blocking collectives, full_plan(): col_total = lax.psum(jnp.sum(col_parts, axis=0)[None, :], 'row')  21.4 us
    psum x2, blocking collectives, combine(): whole = lax.psum(partial_value, 'col')  16 us
    another operation x1, loops' own time, full_plan(): row_parts, col_parts = lax.map(first_pass, indexes)  12.5 us
    another operation x1, loops' own time, full_plan(): products = lax.map(third_pass, indexes)  12.5 us
    another operation x1, loops' own time, full_plan(): second = combine(lax.map(second_pass, indexes).reshape(1, rows), owned)  12.5 us
    dot_general x9, matrix products, kernel_rows(): jnp.einsum('fi,fj->ij', part, col_feat, precision=lax.Precision.HIGHEST)  6.41 us

commit v1 on v0

--- a/solution.py
+++ b/solution.py
@@ -20,7 +20,9 @@
 
 def full_plan(features, block, row_feat, scale):
     owned = features.shape[1]
-    col_feat = lax.all_gather(features, "row", axis=1, tiled=True)
+    col_feat = jnp.concatenate(
+        lax.all_to_all(jnp.stack([features] * lax.axis_size("row")), "row", 0, 0), axis=1
+    )
     row_sq = jnp.sum(row_feat * row_feat, axis=0)
     col_sq = jnp.sum(col_feat * col_feat, axis=0)
     rows = row_feat.shape[1]

time: 167 us -> 142 us (0.85)
  blocking collectives: 106 us -> 71.8 us
  starting transfers between devices: 0 us -> 7.44 us
  waiting for transfers between devices: 0 us -> 1.9 us
    all_gather x1 -> x0, blocking collectives: 32.5 us -> none  [full_plan(): col_feat = lax.all_gather(features, 'row', axis=1, tiled=True)]
    all_to_all x0 -> x1, starting transfers between devices: none -> 7.44 us  [full_plan(): lax.all_to_all(jnp.stack([features] * lax.axis_size('row')), 'row', 0, 0)]
    all_to_all x0 -> x1, waiting for transfers between devices: none -> 1.9 us  [full_plan(): lax.all_to_all(jnp.stack([features] * lax.axis_size('row')), 'row', 0, 0)]
  transfers between devices with their start and end apart: 0 -> 1, of which waited for: 0 -> 1; matrix products, arithmetic and copies ran while one was open for 0% -> 0% of each run, Pallas kernels for 0% -> 0%
where the time goes in v1:
time: 142 us; the launch traced here: 141 us
  blocking collectives  71.8 us (51%)
  loops' own time  37.5 us (26%)
  local copies, waits for them, and re-layouts  15.1 us (11%)
  starting transfers between devices  7.44 us (5%)
  matrix products  6.79 us (5%)
  waiting for transfers between devices  1.9 us (1%)
    all_gather x1, blocking collectives, full_plan(): weighted_col = lax.all_gather(weighted, 'row', axis=1, tiled=True)  30.6 us
    psum x1, blocking collectives, full_plan(): col_total = lax.psum(jnp.sum(col_parts, axis=0)[None, :], 'row')  19.9 us
    psum x2, blocking collectives, combine(): whole = lax.psum(partial_value, 'col')  16 us
    another operation x1, loops' own time, full_plan(): row_parts, col_parts = lax.map(first_pass, indexes)  12.5 us
    another operation x1, loops' own time, full_plan(): products = lax.map(third_pass, indexes)  12.5 us
    another operation x1, loops' own time, full_plan(): second = combine(lax.map(second_pass, indexes).reshape(1, rows), owned)  12.5 us
    all_to_all x1, starting transfers between devices, full_plan(): lax.all_to_all(jnp.stack([features] * lax.axis_size('row')), 'row', 0, 0)  7.44 us
    dot_general x9, matrix products, kernel_rows(): jnp.einsum('fi,fj->ij', part, col_feat, precision=lax.Precision.HIGHEST)  6.41 us
  transfers between devices with their start and end apart: 1, of which 1 were waited for; matrix products, arithmetic and copies ran while one was open for 0% of the time, Pallas kernels for 0%

profile of v1, /device:TPU:0, one launch (start us, length us, event | category | flops | bytes accessed | tf_op | source)
XLA Modules:
  0.0 141.5 jit_solution(8643121587314181985)
XLA Ops:
  0.0 1.4 stack.2
  1.4 7.4 %all-to-all-start = ((f32[8,32,96]{2,1,0:T(8,128)}), f32[8,32,96]{2,1,0:T(8,128)S(1)}, u32[]{:S(2)}, u32[]{:S(2)}) async-start(f32[8,32,96]{2,1,0:T(8,128)} %stack.2), calls=%async_computation | async-start | bytes 262144 | tf_op jit(solution)/shard_map/all_to_all | solution.py:24
  8.8 5.2 %all-gather = f32[4,96,32]{1,2,0:T(8,128)S(1)} all-gather(f32[1,96,32]{1,2,0:T(8,128)S(1)} %bitcast.82), channel_id=1, replica_groups=mesh['row'=8,'col'=4] {'col'}, dimensions={0}, use_global_device_ids=true | all-gather | bytes 61440 | tf_op jit(solution)/shard_map/all_gather | solution.py:72
  14.2 1.9 %all-to-all-done = f32[8,32,96]{2,1,0:T(8,128)S(1)} async-done(((f32[8,32,96]{2,1,0:T(8,128)}), f32[8,32,96]{2,1,0:T(8,128)S(1)}, u32[]{:S(2)}, u32[]{:S(2)}) %all-to-all-start) | async-done | bytes 98336 | tf_op jit(solution)/shard_map/all_to_all | solution.py:24
  16.4 19.3 %while.32 = (s32[]{:T(128)}, f32[3,128]{1,0:T(4,128)S(1)}, f32[3,768]{1,0:T(4,128)S(1)}, s32[3]{0:T(128)S(1)}, s32[3]{0:T(128)S(1)}, /*index=5*/f32[384]{0:T(512...) while((s32[]{:T(128)}, f32[3,128]{1,0:T(4,128)S(1)}, ...), condition=%wide.region_5.6_spmd, body=%wide.region_2.5_spmd.sunk | while | flops 38632584 | bytes 137449 | solution.py:41
  19.2 0.7 dynamic_slice.88
  22.0 0.7 fusion.51
  22.9 0.7 dynamic_slice.87
  25.6 0.7 dynamic_slice.88
  28.4 0.7 fusion.51
  32.0 0.7 dynamic_slice.88
  34.9 0.7 fusion.51
  35.8 19.9 %psum.29 = f32[1,768]{1,0:T(1,128)S(1)} all-reduce(f32[1,768]{1,0:T(1,128)S(1)} %broadcast_in_dim.32), channel_id=1, replica_groups=mesh['row'=8,'col'=4] {'row'}, use_global_device_ids=true, to_apply=%region_8.9 | all-reduce | flops 768 | bytes 6144 | tf_op jit(solution)/shard_map/psum | solution.py:44
  55.7 19.1 %while.33 = (s32[]{:T(128)}, f32[3,128]{1,0:T(4,128)S(1)}, s32[3]{0:T(128)S(1)}, s32[3]{0:T(128)S(1)}, f32[384]{0:T(512)S(1)}, /*index=5*/f32[768]{0:T(1024)S(1)...) while((s32[]{:T(128)}, f32[3,128]{1,0:T(4,128)S(1)}, ...), condition=%wide.region_11.12_spmd, body=%wide.region_9.11_spmd.sunk | while | flops 38633352 | bytes 132337 | solution.py:50
  55.7 0.7 dynamic_slice.91
  58.5 0.7 dynamic_slice.92
  61.3 0.7 fusion.54
  64.8 0.7 dynamic_slice.92
  67.7 0.7 fusion.54
  68.5 0.7 dynamic_slice.91
  71.2 0.7 dynamic_slice.92
  74.0 0.7 fusion.54
  74.9 5.7 %all-reduce = (f32[1,384]{1,0:T(1,128)S(1)}, f32[1,384]{1,0:T(1,128)S(1)}) all-reduce(f32[1,384]{1,0:T(1,128)S(1)} %get-tuple-element.209, f32[1,384]{1,0:T(1,128)S(1)} %get-tuple-element.210), channel_id=1, replica_groups=mesh['row'=8,'col'=4] {'col'}, use_global_device_ids=true, to_apply=%region_12.13 | all-reduce | flops 768 | bytes 6144 | tf_op jit(solution)/shard_map/psum | solution.py:17
  80.6 30.6 %all-gather.1 = bf16[8,96,16]{1,2,0:T(8,128)(2,1)S(1)} all-gather(bf16[1,96,16]{1,2,0:T(8,128)(2,1)S(1)} %fusion.26), channel_id=1, replica_groups=mesh['row'=8,'col'=4] {'row'}, dimensions={0}, use_global_device_ids=true | all-gather | bytes 27648 | tf_op jit(solution)/shard_map/all_gather | solution.py:54
  111.3 19.2 %while.34 = (s32[]{:T(128)}, f32[3,16,128]{2,1,0:T(8,128)S(1)}, s32[3]{0:T(128)S(1)}, s32[3]{0:T(128)S(1)}, f32[384]{0:T(512)S(1)}, /*index=5*/f32[768]{0:T(1024...) while((s32[]{:T(128)}, f32[3,16,128]{2,1,0:T(8,128)S(1)}, ...), condition=%wide.region_14.15_spmd, body=%wide.region_13.14_spmd.sunk | while | flops 41484296 | bytes 546533 | solution.py:61
  114.1 0.7 dynamic_slice.96
  117.7 0.7 dynamic_slice.95
  120.5 0.7 dynamic_slice.96
  124.1 0.7 dynamic_slice.95
  126.9 0.7 dynamic_slice.96
  130.5 10.3 %psum.31 = f32[16,384]{1,0:T(8,128)S(1)} all-reduce(f32[16,384]{1,0:T(8,128)S(1)} %copy_bitcast_fusion), channel_id=1, replica_groups=mesh['row'=8,'col'=4] {'col'}, use_global_device_ids=true, to_apply=%region_15.16 | all-reduce | flops 6144 | bytes 49152 | tf_op jit(solution)/shard_map/psum | solution.py:17
  140.8 0.7 dynamic-slice_multiply_fusion
  (62 shorter events, 6.8 us)
Async XLA Ops:
  1.4 7.5 %copy-start = (f32[32,96]{1,0:T(8,128)S(1)}, f32[32,96]{1,0:T(8,128)}, u32[]{:S(2)}) copy-start(f32[32,96]{1,0:T(8,128)} %param.8) | copy-start | bytes 36868
  1.4 14.8 %all-to-all-start = ((f32[8,32,96]{2,1,0:T(8,128)}), f32[8,32,96]{2,1,0:T(8,128)S(1)}, u32[]{:S(2)}, u32[]{:S(2)}) async-start(f32[8,32,96]{2,1,0:T(8,128)} %stack.2), calls=%async_computation | async-start | bytes 262144 | tf_op jit(solution)/shard_map/all_to_all | solution.py:24
  74.8 5.8 %copy-start.1 = (f32[16,96]{1,0:T(8,128)S(1)}, f32[16,96]{1,0:T(8,128)}, u32[]{:S(2)}) copy-start(f32[16,96]{1,0:T(8,128)} %param.9) | copy-start | bytes 18436
